TPU v7x, 128 devices: a whole 4x4x4 slice. The times are simulated.
128 devices in a mesh: row: 16 (over x, y), col: 8 (over z, core).
Axes of the slice: x: 4, y: 4, z: 4, core: 2. Of those that a mesh axis runs over, the one named last changes fastest.
Arguments:
- signal: float32 [256, 256, 16, 256], P('row', 'col'), may hold values from -40 to 40, as said below
- start_frames: float32 [256, 32], replicated, may hold values from -6 to 6
- start_sends: float32 [16, 8], replicated, may hold values from -6 to 6
- start_rows: float32 [256, 64], replicated, may hold values from -6 to 6
- start_cols: float32 [256, 64], replicated, may hold values from -6 to 6
- rank_frames: int32 [1], replicated, may hold values from 16 to 32
- rank_sends: int32 [1], replicated, may hold values from 4 to 8
Outputs:
- filtered: float32 [256, 256, 16, 256], P('row', 'col')
Inputs may be any that keep to these rules, and one draw needn't show every extreme that they name: `signal`: beamformed samples.
All inputs are finite; a program needn't handle non-finite values.
Results may differ from a plain program's by a relative error of at most 0.0003.
Values sent between devices are 32-bit elements; how exact they have to be, the bound alone decides.
A program may use at most 128 MiB of HBM per device.

v0:
```python
import functools

import jax
import jax.numpy as jnp
from jax import lax
from jax.experimental import pallas as pl
from jax.experimental.pallas import tpu as pltpu
from jax.sharding import PartitionSpec as P

NT = 256
NK = 16
TMAX = 32
KMAX = 8
RS = 64
ITERS = 2
NDEV = 128
ROWS = 16
COLS = 32
LINES = COLS * NK
MESH = pl.DeviceIdType.MESH
F32 = jnp.float32
BF16 = jnp.bfloat16
HIGH = lax.Precision.HIGHEST


def me_index():
    return lax.axis_index("row") * 8 + lax.axis_index("col")


def dot(a, b, over=(1, 0)):
    dims = (((over[0],), (over[1],)), ((), ()))
    return lax.dot_general(a, b, dims, preferred_element_type=F32)


def full_dot(a, b, over=(1, 0)):
    dims = (((over[0],), (over[1],)), ((), ()))
    return lax.dot_general(a, b, dims, precision=HIGH, preferred_element_type=F32)


def halves(x):
    hi = x.astype(BF16)
    return hi, (x - hi.astype(F32)).astype(BF16)


def dot3(a, b, over=(1, 0)):
    a_hi, a_lo = halves(a)
    b_hi, b_lo = halves(b)
    return dot(a_hi, b_hi, over) + dot(a_hi, b_lo, over) + dot(a_lo, b_hi, over)


def self_dot(a):
    hi, lo = halves(a)
    side = dot(hi, lo, (1, 1))
    return dot(hi, hi, (1, 1)) + side + side.T


def remote(src, dst, send, recv, dev):
    return pltpu.make_async_remote_copy(
        src_ref=src, dst_ref=dst, send_sem=send, recv_sem=recv, device_id=dev, device_id_type=MESH
    )


def wait_for(ref, count, sem):
    some = ref.at[pl.ds(0, count)]
    pltpu.make_async_copy(some, some, sem).wait()


HOPS = (0, 1, 2, 1)
CHIPS = sorted(
    [(x, y, z) for x in range(4) for y in range(4) for z in range(4)], key=lambda o: -sum(HOPS[i] for i in o)
)
PEERS = [(x, y, z, k) for x, y, z in CHIPS for k in range(2) if x + y + z + k]


def places():
    row, col = lax.axis_index("row"), lax.axis_index("col")
    x, y, z, k = lax.div(row, 4), lax.rem(row, 4), lax.div(col, 2), lax.rem(col, 2)
    rows = [[lax.rem(x + dx, 4) * 4 + lax.rem(y + dy, 4) for dy in range(4)] for dx in range(4)]
    planes = [lax.rem(z + dz, 4) for dz in range(4)]
    cols = [[planes[dz] * 2 + lax.rem(k + dk, 2) for dk in range(2)] for dz in range(4)]
    return rows, cols, planes, k


def all_sum(where, part, inbox, total, sems):
    rows, cols, planes, k = where
    for place, (dx, dy, dz) in enumerate(CHIPS):
        row, plane = rows[dx][dy], planes[dz]
        copy = remote(
            part.at[row * 4 + plane], inbox.at[2 * place + k], sems.at[0], sems.at[1], (row, plane * 2 + 1)
        )
        if dx + dy + dz:
            copy.start()
        else:
            pl.when(k == 0)(copy.start)

    @pl.when(k == 1)
    def _():
        piece = rows[0][0] * 4 + planes[0]
        wait_for(inbox, NDEV - 1, sems.at[1])
        lanes = [inbox[i] for i in range(4)]
        for i in range(4, NDEV - 1):
            lanes[i % 4] = lanes[i % 4] + inbox[i]
        total[piece] = (lanes[0] + lanes[1]) + (lanes[2] + lanes[3]) + part[piece]
        for dx, dy, dz, dk in PEERS:
            remote(total.at[piece], total.at[piece], sems.at[2], sems.at[3], (rows[dx][dy], cols[dz][dk])).start()
        wait_for(part, 63, sems.at[3])

    @pl.when(k == 0)
    def _():
        wait_for(part, 64, sems.at[3])

    def finish():
        @pl.when(k == 1)
        def _():
            wait_for(part, 63, sems.at[0])
            wait_for(inbox, NDEV - 1, sems.at[2])

        @pl.when(k == 0)
        def _():
            wait_for(part, 64, sems.at[0])

    return finish


def pack(gram, part, extra=None):
    corner = gram[128:, 128:]
    if extra is not None:
        lane = lax.broadcasted_iota(jnp.int32, (NK, 128), 1)
        corner = jnp.concatenate([corner[: 128 - NK], jnp.where(lane < NK, extra, corner[128 - NK :])], axis=0)
    lines = jnp.concatenate([gram[:128, :128], gram[:128, 128:], corner], axis=0)
    for p in range(64):
        part[p] = lines[6 * p : 6 * p + 6]


def unpack(total, stage, gram, extra=None):
    for p in range(64):
        stage[6 * p : 6 * p + 6] = total[p]
    side = stage[128:256]
    gram[:128, :128] = stage[:128]
    gram[:128, 128:] = side
    gram[128:, :128] = side.T
    gram[128:, 128:] = stage[256:]
    if extra is not None:
        extra[...] = stage[384 - NK :, :NK]
        lane = lax.broadcasted_iota(jnp.int32, (NK, 128), 1)
        turned = stage[256:].T[128 - NK :]
        gram[256 - NK :, 128:] = jnp.where(lane < NK, turned, stage[384 - NK :])


def inverse_factor(inner, size):
    groups = size // 8
    lane = lax.broadcasted_iota(jnp.int32, (8, size), 1)
    sub = lax.broadcasted_iota(jnp.int32, (8, size), 0)
    rest = [inner[8 * g : 8 * g + 8] for g in range(groups)]
    inv = [jnp.where(lane == sub + 8 * g, 1.0, 0.0).astype(F32) for g in range(groups)]

    def row(x, j):
        return jnp.broadcast_to(x[j : j + 1], (8, size))

    for b in range(groups):
        cols = [
            [jnp.broadcast_to(rest[g][:, 8 * b + j : 8 * b + j + 1], (8, size)) for g in range(b, groups)]
            for j in range(8)
        ]
        pivots = jnp.ones((8, size), F32)
        for j in range(8):
            pivot = row(cols[j][0], j)
            pivots = jnp.where(sub == j, pivot, pivots)
            scale = 1.0 / pivot
            heads = [row(cols[q][0], j) for q in range(j + 1, 8)]
            rest_row = row(rest[b], j)
            inv_row = row(inv[b], j)
            for g in range(b, groups):
                step = cols[j][g - b] * scale
                if g == b:
                    step = jnp.where(sub > j, step, 0.0)
                for q in range(j + 1, 8):
                    cols[q][g - b] = cols[q][g - b] - step * heads[q - j - 1]
                rest[g] = rest[g] - step * rest_row
                inv[g] = inv[g] - step * inv_row
        inv[b] = inv[b] * lax.rsqrt(pivots)
    return jnp.concatenate(inv, axis=0) if groups > 1 else inv[0]


def next_basis(image):
    lower = inverse_factor(full_dot(image, image, (1, 1)), image.shape[0])
    return full_dot(lower, image)


def orth(gram, basis):
    def step(_, c):
        basis[...] = next_basis(full_dot(basis[...], gram[...]))
        return c

    lax.fori_loop(0, ITERS, step, 0)


def swap(x):
    return pltpu.roll(x, 64, 1)


def regroup(a, b):
    left = lax.broadcasted_iota(jnp.int32, a.shape, 1) < 64
    return jnp.where(left, a, swap(b)), jnp.where(left, swap(a), b)


def main_kernel(
    x_hbm, start_f, start_s, start_r, start_c, rank_f, rank_s,
    xin, mixed_out, frames_out,
    xhi, xlo, acc, side, acc_s, side_s, gram, part_f, part_r, part_c,
    in_f, in_r, in_c, tot_f, tot_r, tot_c, stage, gram_s, bft, bst, brt, bct,
    red, kron, back, send1, recv1, unf, send2, recv2,
    load_sems, start_sems, sems, swap_sems,
):
    me = me_index()
    mine_row, mine_col = lax.axis_index("row"), lax.axis_index("col")
    for r in range(ROWS):
        pltpu.make_async_copy(x_hbm.at[r], xin.at[r], load_sems.at[r]).start()
    starts = [
        pltpu.make_async_copy(start, ref, start_sems.at[i])
        for i, (ref, start) in enumerate(((bft, start_f), (bst, start_s), (brt, start_r), (bct, start_c)))
    ]
    for copy in starts:
        copy.start()
    barrier = pltpu.get_barrier_semaphore()

    where = places()
    rows_of, cols_of = where[0], where[1]
    for dx, dy, dz, dk in PEERS:
        pl.semaphore_signal(barrier, inc=1, device_id=(rows_of[dx][dy], cols_of[dz][dk]), device_id_type=MESH)

    acc[...] = jnp.zeros_like(acc)
    side[...] = jnp.zeros_like(side)
    acc_s[...] = jnp.zeros_like(acc_s)
    side_s[...] = jnp.zeros_like(side_s)
    def gather(r, c):
        pltpu.make_async_copy(x_hbm.at[r], xin.at[r], load_sems.at[r]).wait()
        hi, lo = halves(xin[r])
        xhi[r] = hi
        xlo[r] = lo
        acc[...] += dot(hi, hi, (0, 0))
        side[...] += dot(hi, lo, (0, 0))
        acc_s[...] += dot(hi[:256], hi[:256], (1, 1)) + dot(hi[256:], hi[256:], (1, 1))
        side_s[...] += dot(hi[:256], lo[:256], (1, 1)) + dot(hi[256:], lo[256:], (1, 1))
        return c

    lax.fori_loop(0, ROWS, gather, 0)
    sends = acc_s[...] + side_s[...] + side_s[...].T
    i0 = lax.broadcasted_iota(jnp.int32, (256, 256), 0)
    i1 = lax.broadcasted_iota(jnp.int32, (256, 256), 1)
    sends = jnp.where(i0 // NK == i1 // NK, sends, 0.0).reshape(16, NK, 256).sum(axis=0)
    j0 = lax.broadcasted_iota(jnp.int32, (256, 128), 0)
    j1 = lax.broadcasted_iota(jnp.int32, (256, 128), 1)
    small = full_dot(sends, (j0 % NK == j1).astype(F32))
    pack(acc[...] + side[...] + side[...].T, part_f, small)

    for copy in starts:
        copy.wait()
    pl.semaphore_wait(barrier, NDEV - 1)
    finish_f = all_sum(where, part_f, in_f, tot_f, sems.at[0])

    unpack(tot_f, stage, gram, gram_s)

    def both(_, c):
        image = full_dot(bft[...], gram[...])
        small = full_dot(bst[...], gram_s[...])
        bft[...] = next_basis(image)
        bst[...] = next_basis(small)
        return c

    lax.fori_loop(0, ITERS, both, 0)
    keep_f = lax.broadcasted_iota(jnp.int32, (TMAX, NT), 0) < rank_f[0]
    frames_t = bft[...] * keep_f.astype(F32)
    frames_out[...] = frames_t
    keep_s = lax.broadcasted_iota(jnp.int32, (KMAX, NK), 0) < rank_s[0]
    sends = bst[...] * keep_s.astype(F32)
    a0 = lax.broadcasted_iota(jnp.int32, (KMAX, 256), 0)
    a1 = lax.broadcasted_iota(jnp.int32, (KMAX, 256), 1)
    wide = full_dot(sends, (a0 == a1 // COLS).astype(F32), (0, 0))
    c0 = lax.broadcasted_iota(jnp.int32, (LINES, 256), 0)
    c1 = lax.broadcasted_iota(jnp.int32, (LINES, 256), 1)
    spread = jnp.where(c0 // NK == c1 % COLS, jnp.concatenate([wide] * COLS, axis=0), 0.0)
    kron[0] = spread[:, :128]
    kron[1] = spread[:, 128:]

    f_hi, f_lo = halves(frames_t)
    f_two = jnp.concatenate([f_hi, f_lo], axis=0)
    for r in range(ROWS):
        both_ways = dot(f_two, xhi[r], (1, 1))
        here = both_ways[:TMAX] + both_ways[TMAX:] + dot(f_hi, xlo[r], (1, 1))
        for q in range(4):
            red[q, pl.ds((r // 8) * 256 + r % 8, TMAX, stride=8), :] = here[:, 128 * q : 128 * q + 128]
    own = mine_col * 16 + mine_row
    parity = lax.rem(lax.div(mine_row, 4), 2)
    r_hi, r_lo = halves(jnp.concatenate([red[q] for q in range(4)], axis=1))
    for odd in range(2):
        t = 1 - parity if odd else parity
        k_hi, k_lo = halves(kron[t])
        core = dot(r_hi, k_hi) + dot(r_hi, k_lo) + dot(r_lo, k_hi)
        one, two = regroup(core[:256], core[256:])
        send1[pl.ds(32 * t, 32)] = one.reshape(32, 8, 128)
        send1[pl.ds(64 + 32 * t, 32)] = two.reshape(32, 8, 128)
        if not odd:
            recv1[own] = send1[me]
        for dx, dy, dz, dk in PEERS:
            if dx % 2 == odd:
                row, col = rows_of[dx][dy], cols_of[dz][dk]
                remote(send1.at[row * 8 + col], recv1.at[own], swap_sems.at[0], swap_sems.at[1], (row, col)).start()
    wait_for(recv1, NDEV - 1, swap_sems.at[1])

    for p in range(4):
        lanes = slice(128 * p, 128 * p + 128)
        one, two = regroup(
            recv1[32 * p : 32 * p + 16].reshape(128, 128), recv1[32 * p + 16 : 32 * p + 32].reshape(128, 128)
        )
        both_halves = [one.reshape(16, 1, 8, 128), two.reshape(16, 1, 8, 128)]
        unf[:, lanes] = jnp.concatenate(both_halves, axis=1).reshape(256, 128)
    pack(self_dot(unf[...]), part_r)
    finish_r = all_sum(where, part_r, in_r, tot_r, sems.at[1])
    unpack(tot_r, stage, gram)
    orth(gram, brt)

    second = dot3(brt[...], unf[...])
    turned = second.T.reshape(8, 2, 32, RS)
    cols = [turned[:, e].reshape(256, RS) for e in range(2)]
    pack(self_dot(cols[0]) + self_dot(cols[1]), part_c)
    finish_c = all_sum(where, part_c, in_c, tot_c, sems.at[2])
    unpack(tot_c, stage, gram)
    orth(gram, bct)

    by_col, by_row = bct[...].T, brt[...].T
    backs = []
    for e in range(2):
        third = dot3(bct[...], cols[e])
        backs.append(dot3(by_col, third).reshape(8, 1, 32, RS))
    back[...] = jnp.concatenate(backs, axis=1).reshape(4, 128, RS)
    for near in (2, 1, 3, 0):
        p = where[2][near]
        pairs = dot3(by_row, back[p], (1, 1)).reshape(16, 2, 8, 128)
        one, two = regroup(pairs[:, 0].reshape(128, 128), pairs[:, 1].reshape(128, 128))
        send2[pl.ds(32 * p, 16)] = one.reshape(16, 8, 128)
        send2[pl.ds(32 * p + 16, 16)] = two.reshape(16, 8, 128)
        if near == 0:
            recv2[me] = send2[own]
        for dx, dy, dz, dk in PEERS:
            if dz == near:
                row, col = rows_of[dx][dy], cols_of[dz][dk]
                remote(send2.at[col * 16 + row], recv2.at[me], swap_sems.at[2], swap_sems.at[3], (row, col)).start()
    wait_for(recv2, NDEV - 1, swap_sems.at[3])
    upper, lower = [], []
    for t in range(2):
        one, two = regroup(
            recv2[32 * t : 32 * t + 32].reshape(256, 128), recv2[64 + 32 * t : 96 + 32 * t].reshape(256, 128)
        )
        upper.append(one)
        lower.append(two)
    whole = jnp.concatenate([jnp.concatenate(upper, axis=1), jnp.concatenate(lower, axis=1)], axis=0)
    mixed = dot3(whole, jnp.concatenate([kron[0], kron[1]], axis=1), (1, 1))
    for q in range(4):
        mixed_out[q] = mixed[:, 128 * q : 128 * q + 128]
    for finish in (finish_f, finish_r, finish_c):
        finish()
    wait_for(send1, NDEV - 1, swap_sems.at[0])
    wait_for(send2, NDEV - 1, swap_sems.at[2])


def last_kernel(x_ref, mixed, frames, out_hbm, o_buf, store_sems):
    f_hi, f_lo = halves(frames[...])
    flat = jnp.concatenate([f_hi, f_hi, f_lo], axis=0)
    for r in range(ROWS):
        lines = pl.ds((r // 8) * 256 + r % 8, TMAX, stride=8)
        m_hi, m_lo = halves(jnp.concatenate([mixed[q, lines, :] for q in range(4)], axis=1))
        tall = jnp.concatenate([m_hi, m_lo, m_hi], axis=0)
        o_buf[r] = x_ref[r] - dot(tall, flat, (0, 0))
        pltpu.make_async_copy(o_buf.at[r], out_hbm.at[r], store_sems.at[r]).start()
    for r in range(ROWS):
        pltpu.make_async_copy(o_buf.at[r], out_hbm.at[r], store_sems.at[r]).wait()


def local(signal, start_frames, start_sends, start_rows, start_cols, rank_frames, rank_sends):
    x = signal.reshape(ROWS, LINES, NT)
    vmem = pl.BlockSpec(memory_space=pltpu.VMEM)
    smem = pl.BlockSpec(memory_space=pltpu.SMEM)
    hbm = pl.BlockSpec(memory_space=pltpu.HBM)
    tiles = lambda n: pltpu.VMEM((n, 8, 128), F32)
    flat = lambda *dims: pltpu.VMEM(dims, F32)
    held, mixed, frames = pl.pallas_call(
        main_kernel,
        out_shape=(pltpu.VMEM(x.shape, F32), pltpu.VMEM((4, 512, 128), F32), pltpu.VMEM((TMAX, NT), F32)),
        in_specs=[hbm, hbm, hbm, hbm, hbm, smem, smem],
        out_specs=(vmem, vmem, vmem),
        scratch_shapes=[
            pltpu.VMEM((ROWS, LINES, NT), BF16), pltpu.VMEM((ROWS, LINES, NT), BF16),
            flat(256, 256), flat(256, 256), flat(256, 256), flat(256, 256), flat(256, 256),
            flat(64, 6, 128), flat(64, 6, 128), flat(64, 6, 128),
            flat(NDEV - 1, 6, 128), flat(NDEV - 1, 6, 128), flat(NDEV - 1, 6, 128),
            flat(64, 6, 128), flat(64, 6, 128), flat(64, 6, 128), flat(384, 128), flat(NK, NK),
            flat(TMAX, NT), flat(KMAX, NK), flat(RS, 256), flat(RS, 256),
            flat(4, 512, 128), flat(2, 512, 128), flat(4, 128, RS), tiles(NDEV), tiles(NDEV), flat(256, 512), tiles(NDEV), tiles(NDEV),
            pltpu.SemaphoreType.DMA((ROWS,)), pltpu.SemaphoreType.DMA((4,)), pltpu.SemaphoreType.DMA((3, 4)), pltpu.SemaphoreType.DMA((4,)),
        ],
        compiler_params=pltpu.CompilerParams(
            collective_id=1, has_side_effects=True, vmem_limit_bytes=57573376
        ),
        name="modes",
    )(x, start_frames.T, start_sends.T, start_rows.T, start_cols.T, rank_frames, rank_sends)
    out = pl.pallas_call(
        last_kernel,
        out_shape=jax.ShapeDtypeStruct(x.shape, F32),
        in_specs=[vmem, vmem, vmem],
        out_specs=pl.BlockSpec(memory_space=pl.ANY),
        scratch_shapes=[flat(ROWS, LINES, NT), pltpu.SemaphoreType.DMA((ROWS,))],
        compiler_params=pltpu.CompilerParams(vmem_limit_bytes=24 * 1024 * 1024),
        name="subtract",
    )(held, mixed, frames)
    return out.reshape(signal.shape)


def solution(mesh):
    return jax.shard_map(
        local,
        mesh=mesh,
        in_specs=(P("row", "col", None, None), P(), P(), P(), P(), P(), P()),
        out_specs=P("row", "col", None, None),
        check_vma=False,
    )
```

profile of v0, /device:TPU:1, one launch (start us, length us, event | category | flops | bytes accessed | tf_op | source)
XLA Modules:
  0.0 94.2 jit_solution(17658222217062780443)
XLA Ops:
  1.3 89.0 %modes.1 = (f32[16,512,256]{2,1,0:T(8,128)S(1)}, f32[4,512,128]{2,1,0:T(8,128)S(1)}, f32[32,256]{1,0:T(8,128)S(1)}) custom-call(f32[16,512,256]{2,1,0:T(8,128)} %bitcast.6, f32[32,256]{1,0:T(8,128)} %bitcast.9, f32[8,16]{1,0:T(8,128)} %bitcast.10, f32[64,256]{1,0:T(8,128)} %bitcast.7, f32[64,256]{1,0:T(8,128)} %bitcast.8, s32[1]{0:T(128)S(6)} %copy.8.rank_f, ...), custom_call_target="tpu_custom_call" | custom-call | tf_op jit(solution)/shard_map/modes/pallas_call | solution.py:387
  90.3 3.8 %subtract.1 = f32[16,512,256]{2,1,0:T(8,128)} custom-call(f32[16,512,256]{2,1,0:T(8,128)S(1)} %get-tuple-element.8.x_ref, f32[4,512,128]{2,1,0:T(8,128)S(1)} %get-tuple-element.9.mixed, f32[32,256]{1,0:T(8,128)S(1)} %get-tuple-element.10.frames), custom_call_target="tpu_custom_call" | custom-call | tf_op jit(solution)/shard_map/subtract/pallas_call | solution.py:407
where the time goes:
time: 94.4 us; the launch traced here: 94.2 us
  Pallas kernels  92.8 us (98%)
  between operations  1.47 us (2%)
    pallas_call x1, Pallas kernels, local(): pl.pallas_call(main_kernel, out_shape=(pltpu.VMEM(x.shape, F32), pltpu.VM...  89 us
    pallas_call x1, Pallas kernels, local(): pl.pallas_call(last_kernel, out_shape=jax.ShapeDtypeStruct(x.shape, F32),...  3.76 us

commit v1 on v0

--- a/solution.py
+++ b/solution.py
@@ -43,13 +43,16 @@
 
 
 def dot3(a, b, over=(1, 0)):
-    a_hi, a_lo = halves(a)
-    b_hi, b_lo = halves(b)
+    return split_dot(halves(a), halves(b), over)
+
+
+def split_dot(a, b, over=(1, 0)):
+    (a_hi, a_lo), (b_hi, b_lo) = a, b
     return dot(a_hi, b_hi, over) + dot(a_hi, b_lo, over) + dot(a_lo, b_hi, over)
 
 
-def self_dot(a):
-    hi, lo = halves(a)
+def self_dot(parts):
+    hi, lo = parts
     side = dot(hi, lo, (1, 1))
     return dot(hi, hi, (1, 1)) + side + side.T
 
@@ -157,28 +160,38 @@
     def row(x, j):
         return jnp.broadcast_to(x[j : j + 1], (8, size))
 
+    def column(x, j):
+        return jnp.broadcast_to(x[:, j : j + 1], (8, size))
+
+    diag = [column(rest[0], q) for q in range(8)]
     for b in range(groups):
-        cols = [
-            [jnp.broadcast_to(rest[g][:, 8 * b + j : 8 * b + j + 1], (8, size)) for g in range(b, groups)]
-            for j in range(8)
-        ]
-        pivots = jnp.ones((8, size), F32)
+        below = range(b + 1, groups)
+        cols = {(j, g): column(rest[g], 8 * b + j) for g in below for j in range(8)}
+        ahead = [column(rest[b + 1], 8 * b + 8 + q) for q in range(8)] if below else None
+        roots = jnp.ones((8, size), F32)
         for j in range(8):
-            pivot = row(cols[j][0], j)
-            pivots = jnp.where(sub == j, pivot, pivots)
-            scale = 1.0 / pivot
-            heads = [row(cols[q][0], j) for q in range(j + 1, 8)]
-            rest_row = row(rest[b], j)
-            inv_row = row(inv[b], j)
-            for g in range(b, groups):
-                step = cols[j][g - b] * scale
-                if g == b:
-                    step = jnp.where(sub > j, step, 0.0)
-                for q in range(j + 1, 8):
-                    cols[q][g - b] = cols[q][g - b] - step * heads[q - j - 1]
+            root = lax.rsqrt(row(diag[j], j))
+            scale = root * root
+            roots = jnp.where(sub == j, root, roots)
+            heads = {q: row(diag[q], j) for q in range(j + 1, 8)}
+            rest_row, inv_row = row(rest[b], j), row(inv[b], j)
+            step = jnp.where(sub > j, diag[j] * scale, 0.0)
+            for q in heads:
+                diag[q] = diag[q] - step * heads[q]
+            rest[b] = rest[b] - step * rest_row
+            inv[b] = inv[b] - step * inv_row
+            for g in below:
+                side = cols[j, g]
+                step = side * scale
+                for q in heads:
+                    cols[q, g] = cols[q, g] - step * heads[q]
                 rest[g] = rest[g] - step * rest_row
                 inv[g] = inv[g] - step * inv_row
-        inv[b] = inv[b] * lax.rsqrt(pivots)
+                if g == b + 1:
+                    for q in range(8):
+                        ahead[q] = ahead[q] - step * row(side, q)
+        inv[b] = inv[b] * roots
+        diag = ahead
     return jnp.concatenate(inv, axis=0) if groups > 1 else inv[0]
 
 
@@ -209,7 +222,7 @@
     xin, mixed_out, frames_out,
     xhi, xlo, acc, side, acc_s, side_s, gram, part_f, part_r, part_c,
     in_f, in_r, in_c, tot_f, tot_r, tot_c, stage, gram_s, bft, bst, brt, bct,
-    red, kron, back, send1, recv1, unf, send2, recv2,
+    red, kron_hi, kron_lo, back, send1, recv1, unf_hi, unf_lo, send2, recv2,
     load_sems, start_sems, sems, swap_sems,
 ):
     me = me_index()
@@ -280,8 +293,9 @@
     c0 = lax.broadcasted_iota(jnp.int32, (LINES, 256), 0)
     c1 = lax.broadcasted_iota(jnp.int32, (LINES, 256), 1)
     spread = jnp.where(c0 // NK == c1 % COLS, jnp.concatenate([wide] * COLS, axis=0), 0.0)
-    kron[0] = spread[:, :128]
-    kron[1] = spread[:, 128:]
+    for part, value in zip((kron_hi, kron_lo), halves(spread)):
+        part[0] = value[:, :128]
+        part[1] = value[:, 128:]
 
     f_hi, f_lo = halves(frames_t)
     f_two = jnp.concatenate([f_hi, f_lo], axis=0)
@@ -295,8 +309,8 @@
     r_hi, r_lo = halves(jnp.concatenate([red[q] for q in range(4)], axis=1))
     for odd in range(2):
         t = 1 - parity if odd else parity
-        k_hi, k_lo = halves(kron[t])
-        core = dot(r_hi, k_hi) + dot(r_hi, k_lo) + dot(r_lo, k_hi)
+        twice = dot(r_hi, jnp.concatenate([kron_hi[t], kron_lo[t]], axis=1))
+        core = twice[:, :128] + twice[:, 128:] + dot(r_lo, kron_hi[t])
         one, two = regroup(core[:256], core[256:])
         send1[pl.ds(32 * t, 32)] = one.reshape(32, 8, 128)
         send1[pl.ds(64 + 32 * t, 32)] = two.reshape(32, 8, 128)
@@ -314,29 +328,30 @@
             recv1[32 * p : 32 * p + 16].reshape(128, 128), recv1[32 * p + 16 : 32 * p + 32].reshape(128, 128)
         )
         both_halves = [one.reshape(16, 1, 8, 128), two.reshape(16, 1, 8, 128)]
-        unf[:, lanes] = jnp.concatenate(both_halves, axis=1).reshape(256, 128)
-    pack(self_dot(unf[...]), part_r)
+        unf_hi[:, lanes], unf_lo[:, lanes] = halves(jnp.concatenate(both_halves, axis=1).reshape(256, 128))
+    pack(self_dot((unf_hi[...], unf_lo[...])), part_r)
     finish_r = all_sum(where, part_r, in_r, tot_r, sems.at[1])
     unpack(tot_r, stage, gram)
     orth(gram, brt)
 
-    second = dot3(brt[...], unf[...])
+    second = split_dot(halves(brt[...]), (unf_hi[...], unf_lo[...]))
     turned = second.T.reshape(8, 2, 32, RS)
-    cols = [turned[:, e].reshape(256, RS) for e in range(2)]
+    cols = [halves(turned[:, e].reshape(256, RS)) for e in range(2)]
     pack(self_dot(cols[0]) + self_dot(cols[1]), part_c)
     finish_c = all_sum(where, part_c, in_c, tot_c, sems.at[2])
     unpack(tot_c, stage, gram)
     orth(gram, bct)
 
-    by_col, by_row = bct[...].T, brt[...].T
+    by_col, by_row = halves(bct[...].T), halves(brt[...].T)
+    col_parts = halves(bct[...])
     backs = []
     for e in range(2):
-        third = dot3(bct[...], cols[e])
-        backs.append(dot3(by_col, third).reshape(8, 1, 32, RS))
+        third = split_dot(col_parts, cols[e])
+        backs.append(split_dot(by_col, halves(third)).reshape(8, 1, 32, RS))
     back[...] = jnp.concatenate(backs, axis=1).reshape(4, 128, RS)
     for near in (2, 1, 3, 0):
         p = where[2][near]
-        pairs = dot3(by_row, back[p], (1, 1)).reshape(16, 2, 8, 128)
+        pairs = split_dot(by_row, halves(back[p]), (1, 1)).reshape(16, 2, 8, 128)
         one, two = regroup(pairs[:, 0].reshape(128, 128), pairs[:, 1].reshape(128, 128))
         send2[pl.ds(32 * p, 16)] = one.reshape(16, 8, 128)
         send2[pl.ds(32 * p + 16, 16)] = two.reshape(16, 8, 128)
@@ -355,7 +370,8 @@
         upper.append(one)
         lower.append(two)
     whole = jnp.concatenate([jnp.concatenate(upper, axis=1), jnp.concatenate(lower, axis=1)], axis=0)
-    mixed = dot3(whole, jnp.concatenate([kron[0], kron[1]], axis=1), (1, 1))
+    kron = [jnp.concatenate([part[0], part[1]], axis=1) for part in (kron_hi, kron_lo)]
+    mixed = split_dot(halves(whole), kron, (1, 1))
     for q in range(4):
         mixed_out[q] = mixed[:, 128 * q : 128 * q + 128]
     for finish in (finish_f, finish_r, finish_c):
@@ -384,6 +400,7 @@
     hbm = pl.BlockSpec(memory_space=pltpu.HBM)
     tiles = lambda n: pltpu.VMEM((n, 8, 128), F32)
     flat = lambda *dims: pltpu.VMEM(dims, F32)
+    short = lambda *dims: pltpu.VMEM(dims, BF16)
     held, mixed, frames = pl.pallas_call(
         main_kernel,
         out_shape=(pltpu.VMEM(x.shape, F32), pltpu.VMEM((4, 512, 128), F32), pltpu.VMEM((TMAX, NT), F32)),
@@ -396,7 +413,8 @@
             flat(NDEV - 1, 6, 128), flat(NDEV - 1, 6, 128), flat(NDEV - 1, 6, 128),
             flat(64, 6, 128), flat(64, 6, 128), flat(64, 6, 128), flat(384, 128), flat(NK, NK),
             flat(TMAX, NT), flat(KMAX, NK), flat(RS, 256), flat(RS, 256),
-            flat(4, 512, 128), flat(2, 512, 128), flat(4, 128, RS), tiles(NDEV), tiles(NDEV), flat(256, 512), tiles(NDEV), tiles(NDEV),
+            flat(4, 512, 128), short(2, 512, 128), short(2, 512, 128), flat(4, 128, RS), tiles(NDEV), tiles(NDEV),
+            short(256, 512), short(256, 512), tiles(NDEV), tiles(NDEV),
             pltpu.SemaphoreType.DMA((ROWS,)), pltpu.SemaphoreType.DMA((4,)), pltpu.SemaphoreType.DMA((3, 4)), pltpu.SemaphoreType.DMA((4,)),
         ],
         compiler_params=pltpu.CompilerParams(

time: 94.4 us -> 91.5 us (0.969)
  Pallas kernels: 92.8 us -> 89.9 us
    pallas_call x1, Pallas kernels: 89 us -> 86.1 us  [local(): pl.pallas_call(main_kernel, out_shape=(pltpu.VMEM(x.shape, F32), pltpu.VM...]
where the time goes in v1:
time: 91.5 us; the launch traced here: 91.4 us
  Pallas kernels  89.9 us (98%)
  between operations  1.47 us (2%)
    pallas_call x1, Pallas kernels, local(): pl.pallas_call(main_kernel, out_shape=(pltpu.VMEM(x.shape, F32), pltpu.VM...  86.1 us
    pallas_call x1, Pallas kernels, local(): pl.pallas_call(last_kernel, out_shape=jax.ShapeDtypeStruct(x.shape, F32),...  3.76 us

profile of v1, /device:TPU:1, one launch (start us, length us, event | category | flops | bytes accessed | tf_op | source)
XLA Modules:
  0.0 91.4 jit_solution(14507878186095809812)
XLA Ops:
  1.3 86.1 %modes.1 = (f32[16,512,256]{2,1,0:T(8,128)S(1)}, f32[4,512,128]{2,1,0:T(8,128)S(1)}, f32[32,256]{1,0:T(8,128)S(1)}) custom-call(f32[16,512,256]{2,1,0:T(8,128)} %bitcast.6, f32[32,256]{1,0:T(8,128)} %bitcast.9, f32[8,16]{1,0:T(8,128)} %bitcast.10, f32[64,256]{1,0:T(8,128)} %bitcast.7, f32[64,256]{1,0:T(8,128)} %bitcast.8, s32[1]{0:T(128)S(6)} %copy.8.rank_f, ...), custom_call_target="tpu_custom_call" | custom-call | tf_op jit(solution)/shard_map/modes/pallas_call | solution.py:404
  87.4 3.8 %subtract.1 = f32[16,512,256]{2,1,0:T(8,128)} custom-call(f32[16,512,256]{2,1,0:T(8,128)S(1)} %get-tuple-element.8.x_ref, f32[4,512,128]{2,1,0:T(8,128)S(1)} %get-tuple-element.9.mixed, f32[32,256]{1,0:T(8,128)S(1)} %get-tuple-element.10.frames), custom_call_target="tpu_custom_call" | custom-call | tf_op jit(solution)/shard_map/subtract/pallas_call | solution.py:425

commit v2 on v1

--- a/solution.py
+++ b/solution.py
@@ -195,14 +195,20 @@
     return jnp.concatenate(inv, axis=0) if groups > 1 else inv[0]
 
 
-def next_basis(image):
+def advance(image, gram, going_on):
     lower = inverse_factor(full_dot(image, image, (1, 1)), image.shape[0])
-    return full_dot(lower, image)
-
-
-def orth(gram, basis):
-    def step(_, c):
-        basis[...] = next_basis(full_dot(basis[...], gram[...]))
+    ahead = full_dot(image, gram)
+    return full_dot(lower, jnp.where(going_on, ahead, image))
+
+
+def orth(*pairs):
+    for gram, basis in pairs:
+        basis[...] = full_dot(basis[...], gram[...])
+
+    def step(i, c):
+        values = [advance(basis[...], gram[...], i + 1 < ITERS) for gram, basis in pairs]
+        for (_, basis), value in zip(pairs, values):
+            basis[...] = value
         return c
 
     lax.fori_loop(0, ITERS, step, 0)
@@ -274,14 +280,7 @@
 
     unpack(tot_f, stage, gram, gram_s)
 
-    def both(_, c):
-        image = full_dot(bft[...], gram[...])
-        small = full_dot(bst[...], gram_s[...])
-        bft[...] = next_basis(image)
-        bst[...] = next_basis(small)
-        return c
-
-    lax.fori_loop(0, ITERS, both, 0)
+    orth((gram, bft), (gram_s, bst))
     keep_f = lax.broadcasted_iota(jnp.int32, (TMAX, NT), 0) < rank_f[0]
     frames_t = bft[...] * keep_f.astype(F32)
     frames_out[...] = frames_t
@@ -332,7 +331,7 @@
     pack(self_dot((unf_hi[...], unf_lo[...])), part_r)
     finish_r = all_sum(where, part_r, in_r, tot_r, sems.at[1])
     unpack(tot_r, stage, gram)
-    orth(gram, brt)
+    orth((gram, brt))
 
     second = split_dot(halves(brt[...]), (unf_hi[...], unf_lo[...]))
     turned = second.T.reshape(8, 2, 32, RS)
@@ -340,7 +339,7 @@
     pack(self_dot(cols[0]) + self_dot(cols[1]), part_c)
     finish_c = all_sum(where, part_c, in_c, tot_c, sems.at[2])
     unpack(tot_c, stage, gram)
-    orth(gram, bct)
+    orth((gram, bct))
 
     by_col, by_row = halves(bct[...].T), halves(brt[...].T)
     col_parts = halves(bct[...])

time: 91.5 us -> 90.5 us (0.989)
  Pallas kernels: 89.9 us -> 88.9 us
    pallas_call x1, Pallas kernels: 86.1 us -> 85.2 us  [local(): pl.pallas_call(main_kernel, out_shape=(pltpu.VMEM(x.shape, F32), pltpu.VM...]
where the time goes in v2:
time: 90.5 us; the launch traced here: 90.4 us
  Pallas kernels  88.9 us (98%)
  between operations  1.47 us (2%)
    pallas_call x1, Pallas kernels, local(): pl.pallas_call(main_kernel, out_shape=(pltpu.VMEM(x.shape, F32), pltpu.VM...  85.2 us
    pallas_call x1, Pallas kernels, local(): pl.pallas_call(last_kernel, out_shape=jax.ShapeDtypeStruct(x.shape, F32),...  3.76 us

profile of v2, /device:TPU:1, one launch (start us, length us, event | category | flops | bytes accessed | tf_op | source)
XLA Modules:
  0.0 90.4 jit_solution(3678133652705618539)
XLA Ops:
  1.3 85.2 %modes.1 = (f32[16,512,256]{2,1,0:T(8,128)S(1)}, f32[4,512,128]{2,1,0:T(8,128)S(1)}, f32[32,256]{1,0:T(8,128)S(1)}) custom-call(f32[16,512,256]{2,1,0:T(8,128)} %bitcast.6, f32[32,256]{1,0:T(8,128)} %bitcast.9, f32[8,16]{1,0:T(8,128)} %bitcast.10, f32[64,256]{1,0:T(8,128)} %bitcast.7, f32[64,256]{1,0:T(8,128)} %bitcast.8, s32[1]{0:T(128)S(6)} %copy.8.rank_f, ...), custom_call_target="tpu_custom_call" | custom-call | tf_op jit(solution)/shard_map/modes/pallas_call | solution.py:403
  86.5 3.8 %subtract.1 = f32[16,512,256]{2,1,0:T(8,128)} custom-call(f32[16,512,256]{2,1,0:T(8,128)S(1)} %get-tuple-element.8.x_ref, f32[4,512,128]{2,1,0:T(8,128)S(1)} %get-tuple-element.9.mixed, f32[32,256]{1,0:T(8,128)S(1)} %get-tuple-element.10.frames), custom_call_target="tpu_custom_call" | custom-call | tf_op jit(solution)/shard_map/subtract/pallas_call | solution.py:424

commit v3 on v2

--- a/solution.py
+++ b/solution.py
@@ -88,8 +88,9 @@
     rows, cols, planes, k = where
     for place, (dx, dy, dz) in enumerate(CHIPS):
         row, plane = rows[dx][dy], planes[dz]
+        slot = 2 * place + k if dx + dy + dz else 2 * place
         copy = remote(
-            part.at[row * 4 + plane], inbox.at[2 * place + k], sems.at[0], sems.at[1], (row, plane * 2 + 1)
+            part.at[row * 4 + plane], inbox.at[slot], sems.at[0], sems.at[1], (row, plane * 2 + 1)
         )
         if dx + dy + dz:
             copy.start()
@@ -226,7 +227,7 @@
 def main_kernel(
     x_hbm, start_f, start_s, start_r, start_c, rank_f, rank_s,
     xin, mixed_out, frames_out,
-    xhi, xlo, acc, side, acc_s, side_s, gram, part_f, part_r, part_c,
+    xhi, xlo, acc, side, acc_s, gram, part_f, part_r, part_c,
     in_f, in_r, in_c, tot_f, tot_r, tot_c, stage, gram_s, bft, bst, brt, bct,
     red, kron_hi, kron_lo, back, send1, recv1, unf_hi, unf_lo, send2, recv2,
     load_sems, start_sems, sems, swap_sems,
@@ -251,7 +252,6 @@
     acc[...] = jnp.zeros_like(acc)
     side[...] = jnp.zeros_like(side)
     acc_s[...] = jnp.zeros_like(acc_s)
-    side_s[...] = jnp.zeros_like(side_s)
     def gather(r, c):
         pltpu.make_async_copy(x_hbm.at[r], xin.at[r], load_sems.at[r]).wait()
         hi, lo = halves(xin[r])
@@ -259,17 +259,19 @@
         xlo[r] = lo
         acc[...] += dot(hi, hi, (0, 0))
         side[...] += dot(hi, lo, (0, 0))
-        acc_s[...] += dot(hi[:256], hi[:256], (1, 1)) + dot(hi[256:], hi[256:], (1, 1))
-        side_s[...] += dot(hi[:256], lo[:256], (1, 1)) + dot(hi[256:], lo[256:], (1, 1))
+        block = 0.0
+        for q in range(0, LINES, 128):
+            here = hi[q : q + 128]
+            block += dot(here, jnp.concatenate([here, lo[q : q + 128]], axis=0), (1, 1))
+        acc_s[...] += block
         return c
 
     lax.fori_loop(0, ROWS, gather, 0)
-    sends = acc_s[...] + side_s[...] + side_s[...].T
-    i0 = lax.broadcasted_iota(jnp.int32, (256, 256), 0)
-    i1 = lax.broadcasted_iota(jnp.int32, (256, 256), 1)
-    sends = jnp.where(i0 // NK == i1 // NK, sends, 0.0).reshape(16, NK, 256).sum(axis=0)
-    j0 = lax.broadcasted_iota(jnp.int32, (256, 128), 0)
-    j1 = lax.broadcasted_iota(jnp.int32, (256, 128), 1)
+    mixed_in = acc_s[:, 128:]
+    sends = acc_s[:, :128] + mixed_in + mixed_in.T
+    j0 = lax.broadcasted_iota(jnp.int32, (128, 128), 0)
+    j1 = lax.broadcasted_iota(jnp.int32, (128, 128), 1)
+    sends = jnp.where(j0 // NK == j1 // NK, sends, 0.0).reshape(8, NK, 128).sum(axis=0)
     small = full_dot(sends, (j0 % NK == j1).astype(F32))
     pack(acc[...] + side[...] + side[...].T, part_f, small)
 
@@ -407,7 +409,7 @@
         out_specs=(vmem, vmem, vmem),
         scratch_shapes=[
             pltpu.VMEM((ROWS, LINES, NT), BF16), pltpu.VMEM((ROWS, LINES, NT), BF16),
-            flat(256, 256), flat(256, 256), flat(256, 256), flat(256, 256), flat(256, 256),
+            flat(256, 256), flat(256, 256), flat(128, 256), flat(256, 256),
             flat(64, 6, 128), flat(64, 6, 128), flat(64, 6, 128),
             flat(NDEV - 1, 6, 128), flat(NDEV - 1, 6, 128), flat(NDEV - 1, 6, 128),
             flat(64, 6, 128), flat(64, 6, 128), flat(64, 6, 128), flat(384, 128), flat(NK, NK),

time: 90.5 us -> 90.4 us (level)
  no operation moved by 1% of the time
where the time goes in v3:
time: 90.4 us; the launch traced here: 90.2 us
  Pallas kernels  88.8 us (98%)
  between operations  1.47 us (2%)
    pallas_call x1, Pallas kernels, local(): pl.pallas_call(main_kernel, out_shape=(pltpu.VMEM(x.shape, F32), pltpu.VM...  85 us
    pallas_call x1, Pallas kernels, local(): pl.pallas_call(last_kernel, out_shape=jax.ShapeDtypeStruct(x.shape, F32),...  3.76 us

profile of v3, /device:TPU:1, one launch (start us, length us, event | category | flops | bytes accessed | tf_op | source)
XLA Modules:
  0.0 90.2 jit_solution(6518502620510887418)
XLA Ops:
  1.3 85.0 %modes.1 = (f32[16,512,256]{2,1,0:T(8,128)S(1)}, f32[4,512,128]{2,1,0:T(8,128)S(1)}, f32[32,256]{1,0:T(8,128)S(1)}) custom-call(f32[16,512,256]{2,1,0:T(8,128)} %bitcast.6, f32[32,256]{1,0:T(8,128)} %bitcast.9, f32[8,16]{1,0:T(8,128)} %bitcast.10, f32[64,256]{1,0:T(8,128)} %bitcast.7, f32[64,256]{1,0:T(8,128)} %bitcast.8, s32[1]{0:T(128)S(6)} %copy.8.rank_f, ...), custom_call_target="tpu_custom_call" | custom-call | tf_op jit(solution)/shard_map/modes/pallas_call | solution.py:405
  86.3 3.8 %subtract.1 = f32[16,512,256]{2,1,0:T(8,128)} custom-call(f32[16,512,256]{2,1,0:T(8,128)S(1)} %get-tuple-element.8.x_ref, f32[4,512,128]{2,1,0:T(8,128)S(1)} %get-tuple-element.9.mixed, f32[32,256]{1,0:T(8,128)S(1)} %get-tuple-element.10.frames), custom_call_target="tpu_custom_call" | custom-call | tf_op jit(solution)/shard_map/subtract/pallas_call | solution.py:426

commit v4 on v3

--- a/solution.py
+++ b/solution.py
@@ -204,7 +204,7 @@
 
 def orth(*pairs):
     for gram, basis in pairs:
-        basis[...] = full_dot(basis[...], gram[...])
+        basis[...] = dot3(basis[...], gram[...])
 
     def step(i, c):
         values = [advance(basis[...], gram[...], i + 1 < ITERS) for gram, basis in pairs]

time: 90.4 us -> 90 us (level)
  no operation moved by 1% of the time
where the time goes in v4:
time: 90 us; the launch traced here: 89.9 us
  Pallas kernels  88.4 us (98%)
  between operations  1.47 us (2%)
    pallas_call x1, Pallas kernels, local(): pl.pallas_call(main_kernel, out_shape=(pltpu.VMEM(x.shape, F32), pltpu.VM...  84.7 us
    pallas_call x1, Pallas kernels, local(): pl.pallas_call(last_kernel, out_shape=jax.ShapeDtypeStruct(x.shape, F32),...  3.76 us

profile of v4, /device:TPU:1, one launch (start us, length us, event | category | flops | bytes accessed | tf_op | source)
XLA Modules:
  0.0 89.9 jit_solution(3002178000853209325)
XLA Ops:
  1.3 84.7 %modes.1 = (f32[16,512,256]{2,1,0:T(8,128)S(1)}, f32[4,512,128]{2,1,0:T(8,128)S(1)}, f32[32,256]{1,0:T(8,128)S(1)}) custom-call(f32[16,512,256]{2,1,0:T(8,128)} %bitcast.6, f32[32,256]{1,0:T(8,128)} %bitcast.9, f32[8,16]{1,0:T(8,128)} %bitcast.10, f32[64,256]{1,0:T(8,128)} %bitcast.7, f32[64,256]{1,0:T(8,128)} %bitcast.8, s32[1]{0:T(128)S(6)} %copy.8.rank_f, ...), custom_call_target="tpu_custom_call" | custom-call | tf_op jit(solution)/shard_map/modes/pallas_call | solution.py:405
  86.0 3.8 %subtract.1 = f32[16,512,256]{2,1,0:T(8,128)} custom-call(f32[16,512,256]{2,1,0:T(8,128)S(1)} %get-tuple-element.8.x_ref, f32[4,512,128]{2,1,0:T(8,128)S(1)} %get-tuple-element.9.mixed, f32[32,256]{1,0:T(8,128)S(1)} %get-tuple-element.10.frames), custom_call_target="tpu_custom_call" | custom-call | tf_op jit(solution)/shard_map/subtract/pallas_call | solution.py:426
